TPU v7x, 32 devices: a whole 2x2x4 slice. The times are simulated.
32 devices in a mesh: dp: 16 (over z, x, core), tensor: 2 (over y).
Axes of the slice: x: 2, y: 2, z: 4, core: 2. Of those that a mesh axis runs over, the one named last changes fastest.
Arguments:
- activations: bfloat16 [4096, 2880], P(('dp', 'tensor')), parts along dimension 0, may hold values from -6 to 6
- segment_ids: int32 [4096], P('dp'), parts along dimension 0, may hold values from 0 to 3, as said below
- attn_gain: float32 [2880], replicated, may hold values from 0.1 to 1.9
- qkv_weight: bfloat16 [2880, 5120], P(None, 'tensor'), may hold values from -2 to 2
- out_weight: bfloat16 [4096, 2880], P('tensor'), may hold values from -0.09375 to 0.09375
- ffn_gain: float32 [2880], replicated, may hold values from 0.1 to 1.9
- gate_weight: bfloat16 [2880, 2048], P(None, 'tensor'), may hold values from -0.109375 to 0.109375
- up_weight: bfloat16 [2880, 2048], P(None, 'tensor'), may hold values from -0.109375 to 0.109375
- down_weight: bfloat16 [2048, 2880], P('tensor'), may hold values from -0.125 to 0.125
Outputs:
- layer_out: bfloat16 [4096, 2880], P(('dp', 'tensor')), parts along dimension 0
There are 16 independent parts, one for each index of `dp`. A program takes and returns all parts, laid end to end along the dimension named above; an argument that names none is the same for every part. Nothing has to cross between parts.
Inputs may be any that keep to these rules, and one draw needn't show every extreme that they name: `segment_ids`: segment numbers never fall along the tokens, and each of the four segments holds at least one token.
All inputs are finite; a program needn't handle non-finite values.
Results may differ from a plain program's by a relative error of at most 0.035.
Values may be sent and summed in bfloat16 or wider, within the bound.
No kernel may reach another device: no remote copies, remote signals or barrier semaphores. Data moves between devices by JAX's collectives and lax.ppermute only.
A program may use at most 128 MiB of HBM per device.

v0:
```python
import jax
import jax.numpy as jnp
from jax import lax
from jax.sharding import PartitionSpec as P

HEADS = 64
KV_HEADS = 8
HEAD_DIM = 64


def normalize(rows_in, gain):
    floats = rows_in.astype(jnp.float32)
    mean_square = jnp.mean(floats * floats, axis=-1, keepdims=True)
    return (floats * lax.rsqrt(mean_square + 1e-05) * gain).astype(jnp.bfloat16)


def attend(projected, segment_ids):
    token_count = projected.shape[0]
    group_size = HEADS // KV_HEADS
    heads_view = projected.reshape(token_count, -1, group_size + 2, HEAD_DIM)
    key_rows = heads_view[:, :, group_size]
    value_rows = heads_view[:, :, group_size + 1]
    block_rows = token_count if token_count <= 512 else 512
    block_count = token_count // block_rows
    positions = jnp.arange(token_count, dtype=jnp.int32)

    def one_block(block_index):
        first_row = block_index * block_rows
        query_rows = lax.dynamic_slice_in_dim(heads_view, first_row, block_rows, 0)[
            :, :, :group_size
        ]
        query_pos = first_row + jnp.arange(block_rows, dtype=jnp.int32)
        query_seg = lax.dynamic_slice_in_dim(segment_ids, first_row, block_rows, 0)
        scores = jnp.einsum(
            "sngd,tnd->ngst", query_rows, key_rows, preferred_element_type=jnp.float32
        ) * HEAD_DIM ** (-0.5)
        allowed = (positions[None, :] <= query_pos[:, None]) & (
            segment_ids[None, :] == query_seg[:, None]
        )
        scores = jnp.where(allowed, scores, -1e30)
        row_max = jnp.max(scores, axis=-1, keepdims=True)
        weights = jnp.exp(scores - row_max)
        row_total = jnp.sum(weights, axis=-1, keepdims=True)
        softmax_out = (weights / row_total).astype(jnp.bfloat16)
        mixed = jnp.einsum(
            "ngst,tnd->sngd", softmax_out, value_rows, preferred_element_type=jnp.float32
        )
        return mixed.astype(jnp.bfloat16)

    blocks_out = lax.map(one_block, jnp.arange(block_count, dtype=jnp.int32))
    return blocks_out.reshape(token_count, -1)


def shards(
    activations,
    segment_ids,
    attn_gain,
    qkv_weight,
    out_weight,
    ffn_gain,
    gate_weight,
    up_weight,
    down_weight,
):
    own_rows = activations.shape[0]
    whole_rows = lax.all_gather(activations, "tensor", axis=0, tiled=True)
    projected = jnp.dot(
        normalize(whole_rows, attn_gain), qkv_weight, preferred_element_type=jnp.float32
    ).astype(jnp.bfloat16)
    mixed_heads = attend(projected, segment_ids)
    head_total = lax.psum(
        jnp.dot(mixed_heads, out_weight, preferred_element_type=jnp.float32).astype(jnp.bfloat16),
        "tensor",
    ).astype(jnp.float32)
    resid_whole = (whole_rows.astype(jnp.float32) + head_total).astype(jnp.bfloat16)
    shard_rows = normalize(resid_whole, ffn_gain)
    gate_act = jnp.dot(shard_rows, gate_weight, preferred_element_type=jnp.float32)
    up_act = jnp.dot(shard_rows, up_weight, preferred_element_type=jnp.float32)
    hidden = (jax.nn.silu(gate_act) * up_act).astype(jnp.bfloat16)
    resid_sum = lax.dynamic_slice_in_dim(
        resid_whole, lax.axis_index("tensor") * own_rows, own_rows, 0
    )
    ffn_out = lax.psum_scatter(
        jnp.dot(hidden, down_weight, preferred_element_type=jnp.float32).astype(jnp.bfloat16),
        "tensor",
        scatter_dimension=0,
        tiled=True,
    ).astype(jnp.float32)
    return (resid_sum.astype(jnp.float32) + ffn_out).astype(jnp.bfloat16)


def solution(mesh):
    placed = (
        P(("dp", "tensor"), None),
        P("dp"),
        P(),
        P(None, "tensor"),
        P("tensor", None),
        P(),
        P(None, "tensor"),
        P(None, "tensor"),
        P("tensor", None),
    )
    return jax.shard_map(
        shards, mesh=mesh, in_specs=placed, out_specs=P(("dp", "tensor"), None), check_vma=False
    )
```

profile of v0, /device:TPU:0, one launch (start us, length us, event | category | flops | bytes accessed | tf_op | source)
XLA Modules:
  0.0 167.5 jit_solution(3976080794666431789)
XLA Ops:
  6.5 0.7 all-gather.2.cloned.1.call-update
  7.3 0.0 all-reduce.2.cloned.1.call-start
  7.3 0.9 fusion.25
  8.2 29.5 %all-gather.2.cloned.1.call-done = bf16[256,2880]{0,1:T(8,128)(2,1)} async-done(((bf16[128,2880]{0,1:T(8,128)(2,1)}), bf16[256,2880]{0,1:T(8,128)(2,1)}) %all-gather.2.cloned.1.call-update) | async-done | bytes 1474576 | tf_op jit(solution)/shard_map/all_gather | solution.py:66
  37.7 1.8 %fusion.9 = f32[256]{0:T(256)S(1)} fusion(bf16[256,2880]{0,1:T(8,128)(2,1)} %all-gather.2.cloned.1.call-done), kind=kLoop, calls=%fused_computation.20 | loop fusion | flops 2211584 | bytes 1475584 | tf_op jit(solution)/shard_map/reduce_sum | solution.py:13
  39.5 10.0 %convolution_convert_fusion.2 = bf16[256,2560]{1,0:T(8,128)(2,1)S(1)} fusion(bf16[2880,2560]{1,0:T(8,128)(2,1)} %param.12, bf16[256,2880]{0,1:T(8,128)(2,1)} %all-gather.2.cloned.1.call-done, f32[2880]{0:T(1024)} %param.11, f32[256]{0:T(256)S(1)} %add_rsqrt_fusion.1), kind=kOutput, calls=%fused_computation.14 | convolution fusion | flops 3778478080 | bytes 17543424 | tf_op jit(solution)/shard_map/dot_general | solution.py:67
  49.5 0.6 copy.18
  50.1 1.3 fusion.18
  51.4 0.0 slice-start
  51.4 5.1 %fusion.30 = (f32[4,8,256]{2,1,0:T(8,128)S(1)}, f32[4,8,256,256]{2,3,1,0:T(8,128)}) fusion(f32[4,256,256,8]{2,1,3,0:T(8,128)S(1)} %fusion.18, pred[256,256]{0,1:T(8,128)(4,1)S(1)} %fusion.25), kind=kOutput, calls=%fused_computation.43 | output fusion | flops 12583167 | bytes 16875520 | tf_op jit(solution)/shard_map/while/body/eval_jaxpr/sub | solution.py:42
  56.5 4.4 %fusion.13 = bf16[4,64,8,256]{3,1,2,0:T(8,128)(2,1)S(1)} fusion(f32[4,8,256,256]{2,3,1,0:T(8,128)} %get-tuple-element.20, f32[4,8,256]{2,1,0:T(8,128)S(1)} %get-tuple-element.19, bf16[256,4,10,64]{0,3,2,1:T(8,128)(2,1)S(1)} %bitcast.39), kind=kOutput, calls=%fused_computation.24 | convolution fusion | flops 273154048 | bytes 9601024 | tf_op jit(solution)/shard_map/while/body/eval_jaxpr/ngst,tnd->sngd/dot_general | solution.py:45
  60.9 0.3 slice-done.2
  61.2 4.3 %convolution_convert_fusion = bf16[256,2880]{0,1:T(8,128)(2,1)} fusion(bf16[2048,2880]{0,1:T(8,128)(2,1)S(1)} %bitcast.41, bf16[256,2048]{0,1:T(8,128)(2,1)S(1)} %bitcast.42), kind=kOutput, calls=%fused_computation.12 | convolution fusion | flops 3020636160 | bytes 14319616 | tf_op jit(solution)/shard_map/dot_general | solution.py:72
  65.6 0.0 all-reduce.2.cloned.1.call-update
  65.6 0.2 reduce-scatter.4.cloned.1.call-start
  65.8 49.3 %all-reduce.2.cloned.1.call-done = bf16[256,2880]{0,1:T(8,128)(2,1)} async-done(((bf16[256,2880]{0,1:T(8,128)(2,1)}), bf16[256,2880]{0,1:T(8,128)(2,1)}) %all-reduce.2.cloned.1.call-update) | async-done | bytes 1474576 | tf_op jit(solution)/shard_map/psum | solution.py:71
  115.1 2.0 %fusion.6 = (f32[256]{0:T(256)S(1)}, bf16[256,2880]{0,1:T(8,128)(2,1)S(1)}) fusion(bf16[256,2880]{0,1:T(8,128)(2,1)} %all-reduce.2.cloned.1.call-done, bf16[256,2880]{0,1:T(8,128)(2,1)S(1)} %copy-done), kind=kLoop, calls=%fused_computation.17 | loop fusion | flops 5160704 | bytes 4424704 | tf_op jit(solution)/shard_map/reduce_sum | solution.py:13
  117.2 5.6 %fusion.23 = f32[256,1024]{1,0:T(8,128)} fusion(bf16[2880,1024]{1,0:T(8,128)(2,1)} %param.15, bf16[256,2880]{0,1:T(8,128)(2,1)S(1)} %get-tuple-element.18, f32[2880]{0:T(1024)S(1)} %copy-done.1, f32[256]{0:T(256)S(1)} %add_rsqrt_fusion), kind=kOutput, calls=%fused_computation.33 | convolution fusion | flops 1512898560 | bytes 8433920 | tf_op jit(solution)/shard_map/dot_general | solution.py:77
  122.7 8.3 %convolution_convert_fusion.1 = bf16[256,2880]{0,1:T(8,128)(2,1)S(1)} fusion(bf16[1024,2880]{0,1:T(8,128)(2,1)} %param.17, bf16[2880,1024]{1,0:T(8,128)(2,1)} %param.16, f32[256,1024]{1,0:T(8,128)} %fusion.23, bf16[256,2880]{0,1:T(8,128)(2,1)S(1)} %get-tuple-element.18, f32[2880]{0:T(1024)S(1)} %copy-done.1, f32[256]{0:T(256)S(1)} %add_rsqrt_fusion), kind=kOutput, calls=%fused_computation.13 | convolution fusion | flops 3025158144 | bytes 15806720 | tf_op jit(solution)/shard_map/dot_general | solution.py:84
  131.1 1.7 %copy.25 = bf16[256,2880]{1,0:T(8,128)(2,1)} copy(bf16[256,2880]{0,1:T(8,128)(2,1)S(1)} %convolution_convert_fusion.1) | data formatting | bytes 2949120
  132.8 0.0 reduce-scatter.4.cloned.1.call-update
  132.8 25.6 %reduce-scatter.4.cloned.1.call-done = bf16[128,2880]{1,0:T(8,128)(2,1)} async-done(((bf16[256,2880]{1,0:T(8,128)(2,1)}), bf16[128,2880]{1,0:T(8,128)(2,1)}) %reduce-scatter.4.cloned.1.call-update) | async-done | bytes 737296
  158.4 1.5 copy.26
  159.9 1.1 add_convert_fusion
  (12 shorter events, 0.0 us)
Async XLA Ops:
  6.5 31.1 %all-gather.2.cloned.1.call-start = ((), (), s32[]{:S(2)}) async-start(), calls=%async_computation.1 | async-start | bytes 2211840 | tf_op jit(solution)/shard_map/all_gather | solution.py:66
  7.3 107.9 %all-reduce.2.cloned.1.call-start = ((), (), s32[]{:S(2)}) async-start(), calls=%async_computation.2 | async-start | bytes 2949120 | tf_op jit(solution)/shard_map/psum | solution.py:71
  51.4 9.5 %slice-start = ((s8[11796480]{0:T(1024)(128)(4,1)}), s8[3407872]{0:T(1024)(128)(4,1)S(1)}, s32[]{:S(2)}) async-start(s8[11796480]{0:T(1024)(128)(4,1)} %bitcast.40), calls=%async_computation.4 | async-start | bytes 6815744
  51.4 9.5 %slice-start.1 = ((s8[11796480]{0:T(1024)(128)(4,1)}), s8[4194304]{0:T(1024)(128)(4,1)S(1)}, s32[]{:S(2)}) async-start(s8[11796480]{0:T(1024)(128)(4,1)} %bitcast.40), calls=%async_computation.5 | async-start | bytes 8388608
  56.5 4.7 %slice-start.2 = ((s8[11796480]{0:T(1024)(128)(4,1)}), s8[4194304]{0:T(1024)(128)(4,1)S(1)}, s32[]{:S(2)}) async-start(s8[11796480]{0:T(1024)(128)(4,1)} %bitcast.40), calls=%async_computation.6 | async-start | bytes 8388608
  61.2 53.9 %copy-start = (bf16[256,2880]{0,1:T(8,128)(2,1)S(1)}, bf16[256,2880]{0,1:T(8,128)(2,1)}, u32[]{:S(2)}) copy-start(bf16[256,2880]{0,1:T(8,128)(2,1)} %all-gather.2.cloned.1.call-done) | copy-start | bytes 4423684
  65.6 51.6 %copy-start.1 = (f32[2880]{0:T(1024)S(1)}, f32[2880]{0:T(1024)}, u32[]{:S(2)}) copy-start(f32[2880]{0:T(1024)} %param.14) | copy-start | bytes 34564
  65.6 92.8 %reduce-scatter.4.cloned.1.call-start = ((), (), s32[]{:S(2)}) async-start(), calls=%async_computation.3 | async-start | bytes 2260992
Sparse Core Ops, SparseCore 0:
  8.9 28.7 all-gather.1
  65.7 49.3 all-reduce.1
  132.9 25.4 reduce-scatter.3
where the time goes:
time: 168 us; the launch traced here: 167 us
  waiting for transfers between devices  105 us (62%)
  matrix products  33.9 us (20%)
  between operations  13.2 us (8%)
  other arithmetic  10.8 us (6%)
  local copies, waits for them, and re-layouts  4.19 us (2%)
    psum x1, waiting for transfers between devices, shards(): lax.psum(jnp.dot(mixed_heads, out_weight, preferred_element_type=jnp.floa...  49.3 us
    all_gather x1, waiting for transfers between devices, shards(): whole_rows = lax.all_gather(activations, 'tensor', axis=0, tiled=True)  29.5 us
    unnamed x4, waiting for transfers between devices  26.3 us
    dot_general x1, matrix products, shards(): jnp.dot(normalize(whole_rows, attn_gain), qkv_weight, preferred_element_t...  10 us
    dot_general x1, matrix products, shards(): jnp.dot(hidden, down_weight, preferred_element_type=jnp.float32)  8.33 us
    dot_general x1, matrix products, shards(): jnp.dot(shard_rows, gate_weight, preferred_element_type=jnp.float32)  5.56 us
    sub x1, other arithmetic, one_block(): weights = jnp.exp(scores - row_max)  5.08 us
    dot_general x1, matrix products, one_block(): jnp.einsum('ngst,tnd->sngd', softmax_out, value_rows, preferred_element_t...  4.38 us
  transfers between devices with their start and end apart: 3, of which 3 were waited for; matrix products, arithmetic and copies ran while one was open for 1% of the time, Pallas kernels for 0%

commit v1 on v0

--- a/solution.py
+++ b/solution.py
@@ -1,11 +1,18 @@
+import functools
+
 import jax
 import jax.numpy as jnp
 from jax import lax
+from jax.experimental import pallas as pl
+from jax.experimental.pallas import tpu as pltpu
 from jax.sharding import PartitionSpec as P
 
 HEADS = 64
 KV_HEADS = 8
 HEAD_DIM = 64
+PARTS = 4
+STEPS = 3
+FEED_STEPS = 4
 
 
 def normalize(rows_in, gain):
@@ -89,6 +96,384 @@
     return (resid_sum.astype(jnp.float32) + ffn_out).astype(jnp.bfloat16)
 
 
+def turn(block):
+    return block.astype(jnp.float32).T
+
+
+def row_scale(floats):
+    mean_square = jnp.sum(floats * floats, axis=0, keepdims=True) * (1.0 / floats.shape[0])
+    return lax.rsqrt(mean_square + 1e-05)
+
+
+def hbm():
+    return pl.BlockSpec(memory_space=pl.ANY)
+
+
+def params(mib, steps=0):
+    return pltpu.CompilerParams(
+        vmem_limit_bytes=mib * 2**20, dimension_semantics=("arbitrary",) * steps if steps else None
+    )
+
+
+def project_own_kernel(x_ref, gain_ref, weight_ref, out_ref, rows_ref, scale_ref):
+    @pl.when(pl.program_id(0) == 0)
+    def _():
+        floats = x_ref[...].astype(jnp.float32)
+        scale_ref[...] = jnp.broadcast_to(row_scale(floats), scale_ref.shape)
+        rows_ref[...] = (floats.T * gain_ref[...]).astype(jnp.bfloat16)
+
+    product = jnp.dot(rows_ref[...], weight_ref[...], preferred_element_type=jnp.float32)
+    out_ref[...] = (product.T * scale_ref[:1]).astype(jnp.bfloat16)
+
+
+def project_own(x_t, gain, weight, name):
+    dim, tokens = x_t.shape
+    columns = weight.shape[1]
+    block = (HEADS // KV_HEADS + 2) * HEAD_DIM
+    return pl.pallas_call(
+        project_own_kernel,
+        name=name,
+        grid=(columns // block,),
+        in_specs=[
+            pl.BlockSpec((dim, tokens), lambda i: (0, 0)),
+            pl.BlockSpec((1, dim), lambda i: (0, 0)),
+            pl.BlockSpec((dim, block), lambda i: (0, i)),
+        ],
+        out_specs=pl.BlockSpec((block, tokens), lambda i: (i, 0)),
+        out_shape=jax.ShapeDtypeStruct((columns, tokens), jnp.bfloat16),
+        scratch_shapes=[
+            pltpu.VMEM((tokens, dim), jnp.bfloat16),
+            pltpu.VMEM((8, tokens), jnp.float32),
+        ],
+        compiler_params=params(40, 1),
+    )(x_t, gain, weight)
+
+
+def attend_group(queries_t, keys_t, values_t, bias):
+    heads = queries_t.shape[0] // HEAD_DIM
+    tokens = queries_t.shape[1]
+    side = jnp.concatenate(
+        [queries_t[h * HEAD_DIM:(h + 1) * HEAD_DIM] for h in range(heads)], axis=1
+    )
+    key_rows = turn(keys_t).astype(jnp.bfloat16)
+    scores = jnp.dot(key_rows, side, preferred_element_type=jnp.float32)
+    probs = []
+    for h in range(heads):
+        part = scores[:, h * tokens:(h + 1) * tokens] + bias
+        weights = jnp.exp(part - jnp.max(part, axis=0, keepdims=True))
+        inverse = 1.0 / jnp.sum(weights, axis=0, keepdims=True)
+        probs.append((weights * inverse).astype(jnp.bfloat16))
+    mixed = jnp.dot(values_t, jnp.concatenate(probs, axis=1), preferred_element_type=jnp.float32)
+    mixed = mixed.astype(jnp.bfloat16)
+    return jnp.concatenate([mixed[:, h * tokens:(h + 1) * tokens] for h in range(heads)], axis=0)
+
+
+def attend_own_kernel(count, width, *refs):
+    x_refs = refs[:count]
+    (gain_ref, own_ref, bias_ref, weight_ref, out_weight_ref) = refs[count:count + 5]
+    (rows_ref, scale_ref, kv_ref, mixed_ref, first_ref) = refs[count + 5:count + 10]
+    (weights, out_weights, sems, out_sem) = refs[count + 10:]
+    groups = own_ref.shape[0] // width
+    group_rows = width - 2 * HEAD_DIM
+
+    def fetch(g):
+        return pltpu.make_async_copy(
+            weight_ref.at[:, pl.ds(g * width + group_rows, 2 * HEAD_DIM)], weights.at[g], sems.at[g]
+        )
+
+    out_copy = pltpu.make_async_copy(
+        out_weight_ref.at[pl.ds(0, out_weights.shape[0])], out_weights, out_sem
+    )
+    for g in range(groups):
+        fetch(g).start()
+    out_copy.start()
+    at = 0
+    total = 0.0
+    for x_ref in x_refs:
+        floats = x_ref[...].astype(jnp.float32)
+        total = total + jnp.sum(floats * floats, axis=0, keepdims=True)
+        size = x_ref.shape[0]
+        rows_ref[:, at:at + size] = (floats.T * gain_ref[:, at:at + size]).astype(jnp.bfloat16)
+        at += size
+    scale = lax.rsqrt(total * (1.0 / at) + 1e-05)
+    scale_ref[...] = jnp.broadcast_to(scale, scale_ref.shape)
+    for g in range(groups):
+        fetch(g).wait()
+        product = jnp.dot(rows_ref[...], weights[g], preferred_element_type=jnp.float32)
+        kv_ref[g * 2 * HEAD_DIM:(g + 1) * 2 * HEAD_DIM] = (product.T * scale).astype(jnp.bfloat16)
+
+    def one_group(g, carry):
+        start = pl.multiple_of(g * width, HEAD_DIM)
+        kv_start = pl.multiple_of(g * 2 * HEAD_DIM, HEAD_DIM)
+        queries_t = own_ref[pl.ds(start, group_rows)] * HEAD_DIM**-0.5
+        own_kv = own_ref[pl.ds(pl.multiple_of(start + group_rows, HEAD_DIM), 2 * HEAD_DIM)]
+        peer_kv = kv_ref[pl.ds(kv_start, 2 * HEAD_DIM)]
+        both = jnp.concatenate([own_kv, peer_kv], axis=1)
+        mixed_ref[pl.ds(pl.multiple_of(g * group_rows, HEAD_DIM), group_rows)] = attend_group(
+            queries_t, both[:HEAD_DIM], both[HEAD_DIM:], bias_ref[...]
+        )
+        return carry
+
+    lax.fori_loop(0, groups, one_group, 0)
+    out_copy.wait()
+    first_ref[...] = jnp.dot(
+        out_weights[...], mixed_ref[...], preferred_element_type=jnp.float32
+    ).astype(jnp.bfloat16)
+
+
+def attend_own(x_parts, gain, own_t, bias, weight, out_weight_t, size, name):
+    dim, columns = weight.shape
+    tokens = own_t.shape[1]
+    width = (HEADS // KV_HEADS + 2) * HEAD_DIM
+    groups = columns // width
+    count = len(x_parts)
+    vmem = pl.BlockSpec(memory_space=pltpu.VMEM)
+    mixed_rows = groups * (width - 2 * HEAD_DIM)
+    return pl.pallas_call(
+        functools.partial(attend_own_kernel, count, width),
+        name=name,
+        in_specs=[vmem] * (count + 3) + [hbm(), hbm()],
+        out_specs=[vmem] * 5,
+        out_shape=[
+            jax.ShapeDtypeStruct((tokens, dim), jnp.bfloat16),
+            jax.ShapeDtypeStruct((8, tokens), jnp.float32),
+            jax.ShapeDtypeStruct((groups * 2 * HEAD_DIM, tokens), jnp.bfloat16),
+            jax.ShapeDtypeStruct((mixed_rows, tokens), jnp.bfloat16),
+            jax.ShapeDtypeStruct((size, tokens), jnp.bfloat16),
+        ],
+        scratch_shapes=[
+            pltpu.VMEM((groups, dim, 2 * HEAD_DIM), jnp.bfloat16),
+            pltpu.VMEM((size, mixed_rows), jnp.bfloat16),
+            pltpu.SemaphoreType.DMA((groups,)),
+            pltpu.SemaphoreType.DMA,
+        ],
+        compiler_params=params(40),
+    )(*x_parts, gain, own_t, bias, weight, out_weight_t)
+
+
+def attend_peer_kernel(rows_ref, scale_ref, own_kv_ref, kv_ref, bias_ref, weight_ref, mixed_ref):
+    group_rows = weight_ref.shape[1] - 2 * HEAD_DIM
+    product = jnp.dot(
+        rows_ref[...], weight_ref[:, :group_rows], preferred_element_type=jnp.float32
+    )
+    queries_t = (product.T * scale_ref[:1]).astype(jnp.bfloat16) * HEAD_DIM**-0.5
+    both = jnp.concatenate([own_kv_ref[...], kv_ref[...]], axis=1)
+    mixed_ref[...] = attend_group(queries_t, both[:HEAD_DIM], both[HEAD_DIM:], bias_ref[...])
+
+
+def attend_peer(rows, scale, own_t, kv, bias, weight, name):
+    dim, columns = weight.shape
+    tokens = rows.shape[0]
+    per_group = HEADS // KV_HEADS
+    width = (per_group + 2) * HEAD_DIM
+    groups = columns // width
+    group_rows = per_group * HEAD_DIM
+    kv_at = width // (2 * HEAD_DIM)
+    return pl.pallas_call(
+        attend_peer_kernel,
+        name=name,
+        grid=(groups,),
+        in_specs=[
+            pl.BlockSpec((tokens, dim), lambda g: (0, 0)),
+            pl.BlockSpec((8, tokens), lambda g: (0, 0)),
+            pl.BlockSpec((2 * HEAD_DIM, tokens), lambda g: ((g + 1) * kv_at - 1, 0)),
+            pl.BlockSpec((2 * HEAD_DIM, tokens), lambda g: (g, 0)),
+            pl.BlockSpec(bias.shape, lambda g: (0, 0)),
+            pl.BlockSpec((dim, width), lambda g: (0, g)),
+        ],
+        out_specs=pl.BlockSpec((group_rows, tokens), lambda g: (g, 0)),
+        out_shape=jax.ShapeDtypeStruct((groups * group_rows, tokens), jnp.bfloat16),
+        compiler_params=params(40, 1),
+    )(rows, scale, own_t, kv, bias, weight)
+
+
+def project_out_kernel(mixed_ref, weight_ref, out_ref):
+    out_ref[...] = jnp.dot(
+        weight_ref[...], mixed_ref[...], preferred_element_type=jnp.float32
+    ).astype(jnp.bfloat16)
+
+
+def project_out(mixed_t, weight_t, first_row, size, name):
+    depth, tokens = mixed_t.shape
+    block = size // STEPS
+    first_block = first_row // block
+    return pl.pallas_call(
+        project_out_kernel,
+        name=name,
+        grid=(STEPS,),
+        in_specs=[
+            pl.BlockSpec((depth, tokens), lambda i: (0, 0)),
+            pl.BlockSpec((block, depth), lambda i: (first_block + i, 0)),
+        ],
+        out_specs=pl.BlockSpec((block, tokens), lambda i: (i, 0)),
+        out_shape=jax.ShapeDtypeStruct((size, tokens), jnp.bfloat16),
+        compiler_params=params(40, 1),
+    )(mixed_t, weight_t)
+
+
+def feed_kernel(count, steps, last, *refs):
+    x_refs = refs[:count]
+    mine_refs = refs[count:2 * count]
+    came_refs = refs[2 * count:3 * count]
+    gain_ref, gate_ref, up_ref, down_ref = refs[3 * count:3 * count + 4]
+    outs = refs[3 * count + 4:-4]
+    rows_ref, scale_ref, hidden_ref, resid_ref = refs[-4:]
+    step = pl.program_id(0)
+
+    @pl.when(step == 0)
+    def _():
+        at = 0
+        total = 0.0
+        for x_ref, mine_ref, came_ref in zip(x_refs, mine_refs, came_refs):
+            size = x_ref.shape[0]
+            both = mine_ref[...].astype(jnp.float32) + came_ref[...].astype(jnp.float32)
+            resid = (x_ref[...].astype(jnp.float32) + both).astype(jnp.bfloat16)
+            resid_ref[at:at + size] = resid
+            floats = resid.astype(jnp.float32)
+            total = total + jnp.sum(floats * floats, axis=0, keepdims=True)
+            rows_ref[:, at:at + size] = (floats.T * gain_ref[:, at:at + size]).astype(jnp.bfloat16)
+            at += size
+        scale = lax.rsqrt(total * (1.0 / at) + 1e-05)
+        scale_ref[...] = jnp.broadcast_to(scale, scale_ref.shape)
+
+    @pl.when(step < steps)
+    def _():
+        rows = rows_ref[...]
+        scale = scale_ref[:1]
+        gate = jnp.dot(rows, gate_ref[...], preferred_element_type=jnp.float32).T * scale
+        up = jnp.dot(rows, up_ref[...], preferred_element_type=jnp.float32).T * scale
+        block = gate.shape[0]
+        hidden_ref[pl.ds(pl.multiple_of(step * block, block), block)] = (
+            gate / (1.0 + jnp.exp(-gate)) * up
+        ).astype(jnp.bfloat16)
+
+    for part in range(count):
+        @pl.when(step == steps + part)
+        def _(part=part):
+            product = jnp.dot(
+                down_ref[...], hidden_ref[...], preferred_element_type=jnp.float32
+            ).astype(jnp.bfloat16)
+            if last:
+                size = product.shape[0]
+                resid = resid_ref[part * size:(part + 1) * size].astype(jnp.float32)
+                outs[part][...] = resid + product.astype(jnp.float32)
+            else:
+                outs[part][...] = product
+
+
+def feed(x_parts, mine_parts, came_parts, gain, gate, up, down_t, last, name):
+    count = len(x_parts)
+    size, tokens = x_parts[0].shape
+    dim, units = gate.shape
+    steps = FEED_STEPS
+    block = units // steps
+    whole = pl.BlockSpec((size, tokens), lambda i: (0, 0))
+    column = pl.BlockSpec((dim, block), lambda i: (0, jnp.minimum(i, steps - 1)))
+    return pl.pallas_call(
+        functools.partial(feed_kernel, count, steps, last),
+        name=name,
+        grid=(steps + count,),
+        in_specs=[whole] * (3 * count) + [
+            pl.BlockSpec((1, dim), lambda i: (0, 0)),
+            column,
+            column,
+            pl.BlockSpec((size, units), lambda i: (jnp.maximum(i - steps, 0), 0)),
+        ],
+        out_specs=[whole] * count,
+        out_shape=[
+            jax.ShapeDtypeStruct((size, tokens), jnp.float32 if last else jnp.bfloat16)
+        ] * count,
+        scratch_shapes=[
+            pltpu.VMEM((tokens, dim), jnp.bfloat16),
+            pltpu.VMEM((8, tokens), jnp.float32),
+            pltpu.VMEM((units, tokens), jnp.bfloat16),
+            pltpu.VMEM((dim, tokens), jnp.bfloat16),
+        ],
+        compiler_params=params(40, 1),
+    )(*x_parts, *mine_parts, *came_parts, gain, gate, up, down_t)
+
+
+def finish_kernel(count, *refs):
+    out_ref = refs[-1]
+    size = refs[0].shape[0]
+    for part in range(count):
+        out_ref[part * size:(part + 1) * size] = (
+            refs[part][...] + refs[count + part][...].astype(jnp.float32)
+        ).astype(jnp.bfloat16)
+
+
+def finish(base_parts, came_parts, name):
+    count = len(base_parts)
+    size, tokens = base_parts[0].shape
+    vmem = pl.BlockSpec(memory_space=pltpu.VMEM)
+    return pl.pallas_call(
+        functools.partial(finish_kernel, count),
+        name=name,
+        in_specs=[vmem] * (2 * count),
+        out_specs=vmem,
+        out_shape=jax.ShapeDtypeStruct((count * size, tokens), jnp.bfloat16),
+        compiler_params=params(40),
+    )(*base_parts, *came_parts)
+
+
+def pair_shards(
+    activations,
+    segment_ids,
+    attn_gain,
+    qkv_weight,
+    out_weight,
+    ffn_gain,
+    gate_weight,
+    up_weight,
+    down_weight,
+):
+    tokens, dim = activations.shape
+    size = dim // PARTS
+    at = lax.axis_index("tensor")
+    swap = lambda block: lax.ppermute(block, "tensor", [(0, 1), (1, 0)])
+    x_t = activations.T
+    out_weight_t = out_weight.T
+    down_t = down_weight.T
+    attn_gain = attn_gain.reshape(1, dim)
+    ffn_gain = ffn_gain.reshape(1, dim)
+    x_own = [x_t[i * size:(i + 1) * size] for i in range(PARTS)]
+    x_peer = [swap(part) for part in x_own]
+
+    segments = segment_ids.reshape(2, tokens)
+    own_first = jnp.stack([segments[at], segments[1 - at]]).reshape(-1)
+    offsets = jnp.stack([at, 1 - at]).astype(jnp.int32) * tokens
+    positions = (offsets[:, None] + jnp.arange(tokens, dtype=jnp.int32)[None]).reshape(-1)
+    allowed = (positions[:, None] <= positions[None, :]) & (
+        own_first[:, None] == own_first[None, :]
+    )
+    bias = jnp.where(allowed, 0.0, -1e30).astype(jnp.float32)
+    bias_own, bias_peer = bias[:, :tokens], bias[:, tokens:]
+
+    own_t = project_own(x_t, attn_gain, qkv_weight, "project_own")
+    rows, scale, kv, mixed, first = attend_own(
+        x_peer, attn_gain, own_t, bias_own, qkv_weight, out_weight_t, size, "attend_own"
+    )
+    mine_own = [first] + [
+        project_out(mixed, out_weight_t, i * size, size, f"out_own_{i}") for i in range(1, PARTS)
+    ]
+    came_peer = [swap(part) for part in mine_own]
+    rows, _ = lax.optimization_barrier((rows, mine_own[-1]))
+    mixed_peer = attend_peer(rows, scale, own_t, kv, bias_peer, qkv_weight, "attend_peer")
+    mine_peer = [
+        project_out(mixed_peer, out_weight_t, i * size, size, f"out_peer_{i}")
+        for i in range(PARTS)
+    ]
+    came_own = [swap(part) for part in mine_peer]
+    units_peer = feed(
+        x_peer, mine_peer, came_peer, ffn_gain, gate_weight, up_weight, down_t, False, "feed_peer"
+    )
+    units_came = [swap(part) for part in units_peer]
+    base = feed(
+        x_own, mine_own, came_own, ffn_gain, gate_weight, up_weight, down_t, True, "feed_own"
+    )
+    return finish(base, units_came, "finish").T
+
+
 def solution(mesh):
     placed = (
         P(("dp", "tensor"), None),
@@ -102,5 +487,9 @@
         P("tensor", None),
     )
     return jax.shard_map(
-        shards, mesh=mesh, in_specs=placed, out_specs=P(("dp", "tensor"), None), check_vma=False
-    )
+        pair_shards if mesh.shape["tensor"] == 2 else shards,
+        mesh=mesh,
+        in_specs=placed,
+        out_specs=P(("dp", "tensor"), None),
+        check_vma=False,
+    )

time: 168 us -> 85 us (0.51)
  waiting for transfers between devices: 105 us -> 3.89 us
  Pallas kernels: 0 us -> 55.4 us
  matrix products: 33.9 us -> 0 us
  starting transfers between devices: 0.26 us -> 17.8 us
  between operations: 13.2 us -> 0.4 us
  other arithmetic: 10.8 us -> 0.28 us
  local copies, waits for them, and re-layouts: 4.19 us -> 6.6 us
    pallas_call x0 -> x13, Pallas kernels: none -> 55.4 us  [the longest x2 21.8 us: feed(): pl.pallas_call(functools.partial(feed_kernel, count, steps, last), name=n...]
    psum x1 -> x0, waiting for transfers between devices: 49.3 us -> none  [shards(): lax.psum(jnp.dot(mixed_heads, out_weight, preferred_element_type=jnp.floa...]
    dot_general x6 -> x0, matrix products: 33.9 us -> none  [the longest x1 10 us: shards(): jnp.dot(normalize(whole_rows, attn_gain), qkv_weight, preferred_element_t...]
    all_gather x1 -> x0, waiting for transfers between devices: 29.5 us -> none  [shards(): whole_rows = lax.all_gather(activations, 'tensor', axis=0, tiled=True)]
    unnamed x4 -> x0, waiting for transfers between devices: 26.3 us -> none
    ppermute x0 -> x16, starting transfers between devices: none -> 17.8 us  [pair_shards(): swap = lambda block: lax.ppermute(block, 'tensor', [(0, 1), (1, 0)])]
    sub x1 -> x0, other arithmetic: 5.08 us -> none  [one_block(): weights = jnp.exp(scores - row_max)]
    ppermute x0 -> x16, waiting for transfers between devices: none -> 3.89 us  [pair_shards(): swap = lambda block: lax.ppermute(block, 'tensor', [(0, 1), (1, 0)])]
  transfers between devices with their start and end apart: 3 -> 16, of which waited for: 3 -> 2; matrix products, arithmetic and copies ran while one was open for 1% -> 2% of each run, Pallas kernels for 0% -> 53%
where the time goes in v1:
time: 85 us; the launch traced here: 84.4 us
  Pallas kernels  55.4 us (65%)
  starting transfers between devices  17.8 us (21%)
  local copies, waits for them, and re-layouts  6.6 us (8%)
  waiting for transfers between devices  3.89 us (5%)
    pallas_call x2, Pallas kernels, feed(): pl.pallas_call(functools.partial(feed_kernel, count, steps, last), name=n...  21.8 us
    ppermute x16, starting transfers between devices, pair_shards(): swap = lambda block: lax.ppermute(block, 'tensor', [(0, 1), (1, 0)])  17.8 us
    pallas_call x7, Pallas kernels, project_out(): pl.pallas_call(project_out_kernel, name=name, grid=(STEPS,), in_specs=[pl...  8.74 us
    pallas_call x1, Pallas kernels, attend_peer(): pl.pallas_call(attend_peer_kernel, name=name, grid=(groups,), in_specs=[p...  8.25 us
    pallas_call x1, Pallas kernels, attend_own(): pl.pallas_call(functools.partial(attend_own_kernel, count, width), name=n...  8.05 us
    pallas_call x1, Pallas kernels, project_own(): pl.pallas_call(project_own_kernel, name=name, grid=(columns // block,), i...  7.54 us
    ppermute x16, waiting for transfers between devices, pair_shards(): swap = lambda block: lax.ppermute(block, 'tensor', [(0, 1), (1, 0)])  3.89 us
    unnamed x32, local copies, waits for them, and re-layouts  3.85 us
  transfers between devices with their start and end apart: 16, of which 2 were waited for; matrix products, arithmetic and copies ran while one was open for 2% of the time, Pallas kernels for 53%

profile of v1, /device:TPU:0, one launch (start us, length us, event | category | flops | bytes accessed | tf_op | source)
XLA Modules:
  0.0 84.4 jit_solution(18023130545870866001)
XLA Ops:
  0.0 1.2 %fusion = (bf16[720,128]{1,0:T(8,128)(2,1)S(1)}, bf16[720,128]{1,0:T(8,128)(2,1)S(1)}, bf16[720,128]{1,0:T(8,128)(2,1)S(1)}, bf16[720,128]{1,0:T(8,128)(2,1)S(1)}) fusion(bf16[2880,128]{1,0:T(8,128)(2,1)} %bitcast.23), kind=kLoop, calls=%fused_computation.6 | loop fusion | bytes 1474560 | tf_op jit(solution)/shard_map/slice | solution.py:439
  1.3 3.1 %collective-permute-start = (bf16[720,128]{1,0:T(8,128)(2,1)S(1)}, bf16[720,128]{1,0:T(8,128)(2,1)S(1)}, u32[]{:S(2)}, u32[]{:S(2)}) collective-permute-start(bf16[720,128]{1,0:T(8,128)(2,1)S(1)} %get-tuple-element.36.refs_0_), channel_id=1, source_target_pairs={{0,1},{1,0},{2,3},{3,2},{4,5},{5,4},{6,7},{7,6},{8,9},{9,8},{10,11... | collective-permute-start | bytes 552968 | tf_op jit(solution)/shard_map/ppermute | solution.py:433
  4.4 1.9 %collective-permute-start.2 = (bf16[720,128]{1,0:T(8,128)(2,1)S(1)}, bf16[720,128]{1,0:T(8,128)(2,1)S(1)}, u32[]{:S(2)}, u32[]{:S(2)}) collective-permute-start(bf16[720,128]{1,0:T(8,128)(2,1)S(1)} %get-tuple-element.34.refs_2_), channel_id=1, source_target_pairs={{0,1},{1,0},{2,3},{3,2},{4,5},{5,4},{6,7},{7,6},{8,9},{9,8},{10,11... | collective-permute-start | bytes 552968 | tf_op jit(solution)/shard_map/ppermute | solution.py:433
  8.2 1.1 %copy-done.1 = bf16[128,2880]{0,1:T(8,128)(2,1)S(1)} copy-done((bf16[128,2880]{0,1:T(8,128)(2,1)S(1)}, bf16[128,2880]{0,1:T(8,128)(2,1)}, u32[]{:S(2)}) %copy-start.1) | copy-done | bytes 737304
  9.3 7.5 %project_own.1.refs_5_.own_kv_ref = bf16[2560,128]{1,0:T(8,128)(2,1)S(1)} custom-call(bf16[2880,128]{1,0:T(8,128)(2,1)S(1)} %bitcast.24, f32[1,2880]{1,0:T(1,128)S(1)} %reshape.55.gain_ref.refs_4_, bf16[2880,2560]{1,0:T(8,128)(2,1)} %weight_ref.3), custom_call_target="tpu_custom_call" | custom-call | tf_op jit(solution)/shard_map/project_own/pallas_call | solution.py:133
  17.7 3.1 %collective-permute-done.3.refs_3_ = bf16[720,128]{1,0:T(8,128)(2,1)S(1)} collective-permute-done((bf16[720,128]{1,0:T(8,128)(2,1)S(1)}, bf16[720,128]{1,0:T(8,128)(2,1)S(1)}, u32[]{:S(2)}, u32[]{:S(2)}) %collective-permute-start.3) | collective-permute-done | bytes 184352 | tf_op jit(solution)/shard_map/ppermute | solution.py:433
  20.8 8.0 %attend_own.1 = (bf16[128,2880]{1,0:T(8,128)(2,1)S(1)}, f32[8,128]{1,0:T(8,128)S(1)}, bf16[512,128]{1,0:T(8,128)(2,1)S(1)}, bf16[2048,128]{1,0:T(8,128)(2,1)S(1)}, bf16[720,128]{1,0:T(8,128)(2,1)S(1)}) custom-call(bf16[720,128]{1,0:T(8,128)(2,1)S(1)} %collective-permute-done.refs_0_, bf16[720,128]{1,0:T(8,128)(2,1)S(1)} %collective-permute-done.1.refs_1_, ...), custom_call_target="tpu_custom_call" | custom-call | tf_op jit(solution)/shard_map/attend_own/pallas_call | solution.py:232
  28.9 1.3 %out_own_2.1.refs_6_ = bf16[720,128]{1,0:T(8,128)(2,1)S(1)} custom-call(bf16[2048,128]{1,0:T(8,128)(2,1)S(1)} %get-tuple-element.20.mixed_ref, bf16[2880,2048]{1,0:T(8,128)(2,1)S(1)} %bitcast.14), custom_call_target="tpu_custom_call" | custom-call | tf_op jit(solution)/shard_map/out_own_2/pallas_call | solution.py:300
  30.2 1.8 %collective-permute-start.10 = (bf16[720,128]{1,0:T(8,128)(2,1)S(1)}, bf16[720,128]{1,0:T(8,128)(2,1)S(1)}, u32[]{:S(2)}, u32[]{:S(2)}) collective-permute-start(bf16[720,128]{1,0:T(8,128)(2,1)S(1)} %out_own_2.1.refs_6_), channel_id=1, source_target_pairs={{0,1},{1,0},{2,3},{3,2},{4,5},{5,4},{6,7},{7,6},{8,9},{9,8},{10,11... | collective-permute-start | bytes 552968 | tf_op jit(solution)/shard_map/ppermute | solution.py:433
  32.0 1.2 %out_own_3.1.refs_7_ = bf16[720,128]{1,0:T(8,128)(2,1)S(1)} custom-call(bf16[2048,128]{1,0:T(8,128)(2,1)S(1)} %get-tuple-element.20.mixed_ref, bf16[2880,2048]{1,0:T(8,128)(2,1)S(1)} %bitcast.15), custom_call_target="tpu_custom_call" | custom-call | tf_op jit(solution)/shard_map/out_own_3/pallas_call | solution.py:300
  33.6 1.2 %out_own_1.1.refs_5_ = bf16[720,128]{1,0:T(8,128)(2,1)S(1)} custom-call(bf16[2048,128]{1,0:T(8,128)(2,1)S(1)} %get-tuple-element.20.mixed_ref, bf16[2880,2048]{1,0:T(8,128)(2,1)S(1)} %bitcast.16), custom_call_target="tpu_custom_call" | custom-call | tf_op jit(solution)/shard_map/out_own_1/pallas_call | solution.py:300
  34.9 1.8 %collective-permute-start.9 = (bf16[720,128]{1,0:T(8,128)(2,1)S(1)}, bf16[720,128]{1,0:T(8,128)(2,1)S(1)}, u32[]{:S(2)}, u32[]{:S(2)}) collective-permute-start(bf16[720,128]{1,0:T(8,128)(2,1)S(1)} %out_own_1.1.refs_5_), channel_id=1, source_target_pairs={{0,1},{1,0},{2,3},{3,2},{4,5},{5,4},{6,7},{7,6},{8,9},{9,8},{10,11... | collective-permute-start | bytes 552968 | tf_op jit(solution)/shard_map/ppermute | solution.py:433
  37.0 8.2 %attend_peer.1.mixed_ref = bf16[2048,128]{1,0:T(8,128)(2,1)S(1)} custom-call(bf16[128,2880]{1,0:T(8,128)(2,1)S(1)} %get-tuple-element.22.rows_ref, f32[8,128]{1,0:T(8,128)S(1)} %get-tuple-element.23.scale_ref, bf16[2560,128]{1,0:T(8,128)(2,1)S(1)} %project_own.1.refs_5_.own_kv_ref, bf16[512,128]{1,0:T(8,128)(2,1)S(1)} %get-tuple-element.24.kv_ref, ...), custom_call_target="tpu_custom_call" | custom-call | tf_op jit(solution)/shard_map/attend_peer/pallas_call | solution.py:272
  45.2 1.3 %out_peer_0.1.refs_4_ = bf16[720,128]{1,0:T(8,128)(2,1)S(1)} custom-call(bf16[2048,128]{1,0:T(8,128)(2,1)S(1)} %attend_peer.1.mixed_ref, bf16[2880,2048]{1,0:T(8,128)(2,1)S(1)} %bitcast.17), custom_call_target="tpu_custom_call" | custom-call | tf_op jit(solution)/shard_map/out_peer_0/pallas_call | solution.py:300
  46.5 1.8 %collective-permute-start.4 = (bf16[720,128]{1,0:T(8,128)(2,1)S(1)}, bf16[720,128]{1,0:T(8,128)(2,1)S(1)}, u32[]{:S(2)}, u32[]{:S(2)}) collective-permute-start(bf16[720,128]{1,0:T(8,128)(2,1)S(1)} %out_peer_0.1.refs_4_), channel_id=1, source_target_pairs={{0,1},{1,0},{2,3},{3,2},{4,5},{5,4},{6,7},{7,6},{8,9},{9,8},{10,11... | collective-permute-start | bytes 552968 | tf_op jit(solution)/shard_map/ppermute | solution.py:433
  48.3 1.2 %out_peer_1.1.refs_5_ = bf16[720,128]{1,0:T(8,128)(2,1)S(1)} custom-call(bf16[2048,128]{1,0:T(8,128)(2,1)S(1)} %attend_peer.1.mixed_ref, bf16[2880,2048]{1,0:T(8,128)(2,1)S(1)} %bitcast.18), custom_call_target="tpu_custom_call" | custom-call | tf_op jit(solution)/shard_map/out_peer_1/pallas_call | solution.py:300
  49.9 1.2 %out_peer_2.1.refs_6_ = bf16[720,128]{1,0:T(8,128)(2,1)S(1)} custom-call(bf16[2048,128]{1,0:T(8,128)(2,1)S(1)} %attend_peer.1.mixed_ref, bf16[2880,2048]{1,0:T(8,128)(2,1)S(1)} %bitcast.19), custom_call_target="tpu_custom_call" | custom-call | tf_op jit(solution)/shard_map/out_peer_2/pallas_call | solution.py:300
  51.2 1.8 %collective-permute-start.6 = (bf16[720,128]{1,0:T(8,128)(2,1)S(1)}, bf16[720,128]{1,0:T(8,128)(2,1)S(1)}, u32[]{:S(2)}, u32[]{:S(2)}) collective-permute-start(bf16[720,128]{1,0:T(8,128)(2,1)S(1)} %out_peer_2.1.refs_6_), channel_id=1, source_target_pairs={{0,1},{1,0},{2,3},{3,2},{4,5},{5,4},{6,7},{7,6},{8,9},{9,8},{10,11... | collective-permute-start | bytes 552968 | tf_op jit(solution)/shard_map/ppermute | solution.py:433
  53.0 1.3 %out_peer_3.1.refs_7_ = bf16[720,128]{1,0:T(8,128)(2,1)S(1)} custom-call(bf16[2048,128]{1,0:T(8,128)(2,1)S(1)} %attend_peer.1.mixed_ref, bf16[2880,2048]{1,0:T(8,128)(2,1)S(1)} %bitcast.20), custom_call_target="tpu_custom_call" | custom-call | tf_op jit(solution)/shard_map/out_peer_3/pallas_call | solution.py:300
  54.7 10.9 %feed_peer.1 = (bf16[720,128]{1,0:T(8,128)(2,1)S(1)}, bf16[720,128]{1,0:T(8,128)(2,1)S(1)}, bf16[720,128]{1,0:T(8,128)(2,1)S(1)}, bf16[720,128]{1,0:T(8,128)(2,1)S(1)}) custom-call(bf16[720,128]{1,0:T(8,128)(2,1)S(1)} %collective-permute-done.refs_0_, bf16[720,128]{1,0:T(8,128)(2,1)S(1)} %collective-permute-done.1.refs_1_, ...), custom_call_target="tpu_custom_call" | custom-call | tf_op jit(solution)/shard_map/feed_peer/pallas_call | solution.py:372
  65.6 1.8 %collective-permute-start.12 = (bf16[720,128]{1,0:T(8,128)(2,1)S(1)}, bf16[720,128]{1,0:T(8,128)(2,1)S(1)}, u32[]{:S(2)}, u32[]{:S(2)}) collective-permute-start(bf16[720,128]{1,0:T(8,128)(2,1)S(1)} %get-tuple-element.29), channel_id=1, source_target_pairs={{0,1},{1,0},{2,3},{3,2},{4,5},{5,4},{6,7},{7,6},{8,9},{9,8},{10,11... | collective-permute-start | bytes 552968 | tf_op jit(solution)/shard_map/ppermute | solution.py:433
  67.7 1.7 %collective-permute-start.14 = (bf16[720,128]{1,0:T(8,128)(2,1)S(1)}, bf16[720,128]{1,0:T(8,128)(2,1)S(1)}, u32[]{:S(2)}, u32[]{:S(2)}) collective-permute-start(bf16[720,128]{1,0:T(8,128)(2,1)S(1)} %get-tuple-element.31), channel_id=1, source_target_pairs={{0,1},{1,0},{2,3},{3,2},{4,5},{5,4},{6,7},{7,6},{8,9},{9,8},{10,11... | collective-permute-start | bytes 552968 | tf_op jit(solution)/shard_map/ppermute | solution.py:433
  69.8 2.7 %copy-done = bf16[2880,1024]{1,0:T(8,128)(2,1)S(1)} copy-done((bf16[2880,1024]{1,0:T(8,128)(2,1)S(1)}, bf16[2880,1024]{1,0:T(8,128)(2,1)}, u32[]{:S(2)}) %copy-start) | copy-done | bytes 5898264
  72.5 10.8 %feed_own.1 = (f32[720,128]{1,0:T(8,128)S(1)}, f32[720,128]{1,0:T(8,128)S(1)}, f32[720,128]{1,0:T(8,128)S(1)}, f32[720,128]{1,0:T(8,128)S(1)}) custom-call(bf16[720,128]{1,0:T(8,128)(2,1)S(1)} %copy-done.9, bf16[720,128]{1,0:T(8,128)(2,1)S(1)} %copy-done.7, bf16[720,128]{1,0:T(8,128)(2,1)S(1)} %copy-done.5, bf16[720,128]{1,0:T(8,128)(2,1)S(1)} %copy-done.3, ...), custom_call_target="tpu_custom_call" | custom-call | tf_op jit(solution)/shard_map/feed_own/pallas_call | solution.py:372
  (63 shorter events, 5.8 us)
Async XLA Ops:
  1.2 15.6 %copy-start.2 = (bf16[720,128]{1,0:T(8,128)(2,1)}, bf16[720,128]{1,0:T(8,128)(2,1)S(1)}, u32[]{:S(2)}) copy-start(bf16[720,128]{1,0:T(8,128)(2,1)S(1)} %get-tuple-element.33.refs_3_) | copy-start | bytes 552964
  1.3 15.6 %copy-start.4 = (bf16[720,128]{1,0:T(8,128)(2,1)}, bf16[720,128]{1,0:T(8,128)(2,1)S(1)}, u32[]{:S(2)}) copy-start(bf16[720,128]{1,0:T(8,128)(2,1)S(1)} %get-tuple-element.34.refs_2_) | copy-start | bytes 552964
  1.3 15.6 %copy-start.6 = (bf16[720,128]{1,0:T(8,128)(2,1)}, bf16[720,128]{1,0:T(8,128)(2,1)S(1)}, u32[]{:S(2)}) copy-start(bf16[720,128]{1,0:T(8,128)(2,1)S(1)} %get-tuple-element.35.refs_1_) | copy-start | bytes 552964
  1.3 15.6 %copy-start.8 = (bf16[720,128]{1,0:T(8,128)(2,1)}, bf16[720,128]{1,0:T(8,128)(2,1)S(1)}, u32[]{:S(2)}) copy-start(bf16[720,128]{1,0:T(8,128)(2,1)S(1)} %get-tuple-element.36.refs_0_) | copy-start | bytes 552964
  1.3 15.7 %collective-permute-start = (bf16[720,128]{1,0:T(8,128)(2,1)S(1)}, bf16[720,128]{1,0:T(8,128)(2,1)S(1)}, u32[]{:S(2)}, u32[]{:S(2)}) collective-permute-start(bf16[720,128]{1,0:T(8,128)(2,1)S(1)} %get-tuple-element.36.refs_0_), channel_id=1, source_target_pairs={{0,1},{1,0},{2,3},{3,2},{4,5},{5,4},{6,7},{7,6},{8,9},{9,8},{10,11... | collective-permute-start | bytes 552968 | tf_op jit(solution)/shard_map/ppermute | solution.py:433
  4.4 12.6 %collective-permute-start.1 = (bf16[720,128]{1,0:T(8,128)(2,1)S(1)}, bf16[720,128]{1,0:T(8,128)(2,1)S(1)}, u32[]{:S(2)}, u32[]{:S(2)}) collective-permute-start(bf16[720,128]{1,0:T(8,128)(2,1)S(1)} %get-tuple-element.35.refs_1_), channel_id=1, source_target_pairs={{0,1},{1,0},{2,3},{3,2},{4,5},{5,4},{6,7},{7,6},{8,9},{9,8},{10,11... | collective-permute-start | bytes 552968 | tf_op jit(solution)/shard_map/ppermute | solution.py:433
  4.4 13.3 %collective-permute-start.2 = (bf16[720,128]{1,0:T(8,128)(2,1)S(1)}, bf16[720,128]{1,0:T(8,128)(2,1)S(1)}, u32[]{:S(2)}, u32[]{:S(2)}) collective-permute-start(bf16[720,128]{1,0:T(8,128)(2,1)S(1)} %get-tuple-element.34.refs_2_), channel_id=1, source_target_pairs={{0,1},{1,0},{2,3},{3,2},{4,5},{5,4},{6,7},{7,6},{8,9},{9,8},{10,11... | collective-permute-start | bytes 552968 | tf_op jit(solution)/shard_map/ppermute | solution.py:433
  6.4 14.5 %collective-permute-start.3 = (bf16[720,128]{1,0:T(8,128)(2,1)S(1)}, bf16[720,128]{1,0:T(8,128)(2,1)S(1)}, u32[]{:S(2)}, u32[]{:S(2)}) collective-permute-start(bf16[720,128]{1,0:T(8,128)(2,1)S(1)} %get-tuple-element.33.refs_3_), channel_id=1, source_target_pairs={{0,1},{1,0},{2,3},{3,2},{4,5},{5,4},{6,7},{7,6},{8,9},{9,8},{10,11... | collective-permute-start | bytes 552968 | tf_op jit(solution)/shard_map/ppermute | solution.py:433
  30.2 19.3 %collective-permute-start.10 = (bf16[720,128]{1,0:T(8,128)(2,1)S(1)}, bf16[720,128]{1,0:T(8,128)(2,1)S(1)}, u32[]{:S(2)}, u32[]{:S(2)}) collective-permute-start(bf16[720,128]{1,0:T(8,128)(2,1)S(1)} %out_own_2.1.refs_6_), channel_id=1, source_target_pairs={{0,1},{1,0},{2,3},{3,2},{4,5},{5,4},{6,7},{7,6},{8,9},{9,8},{10,11... | collective-permute-start | bytes 552968 | tf_op jit(solution)/shard_map/ppermute | solution.py:433
  33.3 17.9 %collective-permute-start.11 = (bf16[720,128]{1,0:T(8,128)(2,1)S(1)}, bf16[720,128]{1,0:T(8,128)(2,1)S(1)}, u32[]{:S(2)}, u32[]{:S(2)}) collective-permute-start(bf16[720,128]{1,0:T(8,128)(2,1)S(1)} %out_own_3.1.refs_7_), channel_id=1, source_target_pairs={{0,1},{1,0},{2,3},{3,2},{4,5},{5,4},{6,7},{7,6},{8,9},{9,8},{10,11... | collective-permute-start | bytes 552968 | tf_op jit(solution)/shard_map/ppermute | solution.py:433
  34.9 19.4 %collective-permute-start.9 = (bf16[720,128]{1,0:T(8,128)(2,1)S(1)}, bf16[720,128]{1,0:T(8,128)(2,1)S(1)}, u32[]{:S(2)}, u32[]{:S(2)}) collective-permute-start(bf16[720,128]{1,0:T(8,128)(2,1)S(1)} %out_own_1.1.refs_5_), channel_id=1, source_target_pairs={{0,1},{1,0},{2,3},{3,2},{4,5},{5,4},{6,7},{7,6},{8,9},{9,8},{10,11... | collective-permute-start | bytes 552968 | tf_op jit(solution)/shard_map/ppermute | solution.py:433
  36.7 18.0 %collective-permute-start.8 = (bf16[720,128]{1,0:T(8,128)(2,1)S(1)}, bf16[720,128]{1,0:T(8,128)(2,1)S(1)}, u32[]{:S(2)}, u32[]{:S(2)}) collective-permute-start(bf16[720,128]{1,0:T(8,128)(2,1)S(1)} %get-tuple-element.19.refs_4_), channel_id=1, source_target_pairs={{0,1},{1,0},{2,3},{3,2},{4,5},{5,4},{6,7},{7,6},{8,9},{9,8},{10,11... | collective-permute-start | bytes 552968 | tf_op jit(solution)/shard_map/ppermute | solution.py:433
  46.5 20.9 %collective-permute-start.4 = (bf16[720,128]{1,0:T(8,128)(2,1)S(1)}, bf16[720,128]{1,0:T(8,128)(2,1)S(1)}, u32[]{:S(2)}, u32[]{:S(2)}) collective-permute-start(bf16[720,128]{1,0:T(8,128)(2,1)S(1)} %out_peer_0.1.refs_4_), channel_id=1, source_target_pairs={{0,1},{1,0},{2,3},{3,2},{4,5},{5,4},{6,7},{7,6},{8,9},{9,8},{10,11... | collective-permute-start | bytes 552968 | tf_op jit(solution)/shard_map/ppermute | solution.py:433
  49.6 18.2 %collective-permute-start.5 = (bf16[720,128]{1,0:T(8,128)(2,1)S(1)}, bf16[720,128]{1,0:T(8,128)(2,1)S(1)}, u32[]{:S(2)}, u32[]{:S(2)}) collective-permute-start(bf16[720,128]{1,0:T(8,128)(2,1)S(1)} %out_peer_1.1.refs_5_), channel_id=1, source_target_pairs={{0,1},{1,0},{2,3},{3,2},{4,5},{5,4},{6,7},{7,6},{8,9},{9,8},{10,11... | collective-permute-start | bytes 552968 | tf_op jit(solution)/shard_map/ppermute | solution.py:433
  51.2 18.3 %collective-permute-start.6 = (bf16[720,128]{1,0:T(8,128)(2,1)S(1)}, bf16[720,128]{1,0:T(8,128)(2,1)S(1)}, u32[]{:S(2)}, u32[]{:S(2)}) collective-permute-start(bf16[720,128]{1,0:T(8,128)(2,1)S(1)} %out_peer_2.1.refs_6_), channel_id=1, source_target_pairs={{0,1},{1,0},{2,3},{3,2},{4,5},{5,4},{6,7},{7,6},{8,9},{9,8},{10,11... | collective-permute-start | bytes 552968 | tf_op jit(solution)/shard_map/ppermute | solution.py:433
  54.3 15.5 %collective-permute-start.7 = (bf16[720,128]{1,0:T(8,128)(2,1)S(1)}, bf16[720,128]{1,0:T(8,128)(2,1)S(1)}, u32[]{:S(2)}, u32[]{:S(2)}) collective-permute-start(bf16[720,128]{1,0:T(8,128)(2,1)S(1)} %out_peer_3.1.refs_7_), channel_id=1, source_target_pairs={{0,1},{1,0},{2,3},{3,2},{4,5},{5,4},{6,7},{7,6},{8,9},{9,8},{10,11... | collective-permute-start | bytes 552968 | tf_op jit(solution)/shard_map/ppermute | solution.py:433
  54.6 15.1 %copy-start.3 = (bf16[720,128]{1,0:T(8,128)(2,1)S(1)}, bf16[720,128]{1,0:T(8,128)(2,1)}, u32[]{:S(2)}) copy-start(bf16[720,128]{1,0:T(8,128)(2,1)} %copy-done.2) | copy-start | bytes 552964
  54.7 15.1 %copy-start.5 = (bf16[720,128]{1,0:T(8,128)(2,1)S(1)}, bf16[720,128]{1,0:T(8,128)(2,1)}, u32[]{:S(2)}) copy-start(bf16[720,128]{1,0:T(8,128)(2,1)} %copy-done.4) | copy-start | bytes 552964
  54.7 15.1 %copy-start.7 = (bf16[720,128]{1,0:T(8,128)(2,1)S(1)}, bf16[720,128]{1,0:T(8,128)(2,1)}, u32[]{:S(2)}) copy-start(bf16[720,128]{1,0:T(8,128)(2,1)} %copy-done.6) | copy-start | bytes 552964
  54.7 15.1 %copy-start.9 = (bf16[720,128]{1,0:T(8,128)(2,1)S(1)}, bf16[720,128]{1,0:T(8,128)(2,1)}, u32[]{:S(2)}) copy-start(bf16[720,128]{1,0:T(8,128)(2,1)} %copy-done.8) | copy-start | bytes 552964
  65.6 17.7 %collective-permute-start.12 = (bf16[720,128]{1,0:T(8,128)(2,1)S(1)}, bf16[720,128]{1,0:T(8,128)(2,1)S(1)}, u32[]{:S(2)}, u32[]{:S(2)}) collective-permute-start(bf16[720,128]{1,0:T(8,128)(2,1)S(1)} %get-tuple-element.29), channel_id=1, source_target_pairs={{0,1},{1,0},{2,3},{3,2},{4,5},{5,4},{6,7},{7,6},{8,9},{9,8},{10,11... | collective-permute-start | bytes 552968 | tf_op jit(solution)/shard_map/ppermute | solution.py:433
  67.4 15.9 %collective-permute-start.13 = (bf16[720,128]{1,0:T(8,128)(2,1)S(1)}, bf16[720,128]{1,0:T(8,128)(2,1)S(1)}, u32[]{:S(2)}, u32[]{:S(2)}) collective-permute-start(bf16[720,128]{1,0:T(8,128)(2,1)S(1)} %get-tuple-element.30), channel_id=1, source_target_pairs={{0,1},{1,0},{2,3},{3,2},{4,5},{5,4},{6,7},{7,6},{8,9},{9,8},{10,11... | collective-permute-start | bytes 552968 | tf_op jit(solution)/shard_map/ppermute | solution.py:433
  67.7 15.6 %collective-permute-start.14 = (bf16[720,128]{1,0:T(8,128)(2,1)S(1)}, bf16[720,128]{1,0:T(8,128)(2,1)S(1)}, u32[]{:S(2)}, u32[]{:S(2)}) collective-permute-start(bf16[720,128]{1,0:T(8,128)(2,1)S(1)} %get-tuple-element.31), channel_id=1, source_target_pairs={{0,1},{1,0},{2,3},{3,2},{4,5},{5,4},{6,7},{7,6},{8,9},{9,8},{10,11... | collective-permute-start | bytes 552968 | tf_op jit(solution)/shard_map/ppermute | solution.py:433
  69.5 13.9 %collective-permute-start.15 = (bf16[720,128]{1,0:T(8,128)(2,1)S(1)}, bf16[720,128]{1,0:T(8,128)(2,1)S(1)}, u32[]{:S(2)}, u32[]{:S(2)}) collective-permute-start(bf16[720,128]{1,0:T(8,128)(2,1)S(1)} %get-tuple-element.32), channel_id=1, source_target_pairs={{0,1},{1,0},{2,3},{3,2},{4,5},{5,4},{6,7},{7,6},{8,9},{9,8},{10,11... | collective-permute-start | bytes 552968 | tf_op jit(solution)/shard_map/ppermute | solution.py:433
  (8 other events, 43.6 us)
